TPU v7x, 32 devices: a whole 2x2x4 slice. The times are simulated.
32 devices in a mesh: grp: 4 (over x, core), sub: 8 (over z, y).
Axes of the slice: x: 2, y: 2, z: 4, core: 2. Of those that a mesh axis runs over, the one named last changes fastest.
Arguments:
- fine_res: float32 [3, 131072], P(None, ('grp', 'sub'))
- node_map: int32 [2, 131072], P(None, ('grp', 'sub')), may hold values from 0 to 16383, as said below
- connect: int32 [4, 32768], P(None, 'sub'), may hold values from 0 to 16383, as said below
- grads: float32 [3, 3, 32768], P(None, None, 'sub'), may hold values from -6 to 6
- moduli: float32 [2, 32768], P(None, 'sub'), may hold values from 0.2 to 2
- mass: float32 [16384], P('sub'), may hold values from 0.5 to 4
Outputs:
- correction: float32 [3, 131072], P(None, ('grp', 'sub'))
Inputs may be any that keep to these rules, and one draw needn't show every extreme that they name: `node_map`: fine nodes 4096 * b to 4096 * (b + 1) - 1 lie in column c = b % 8; both their entries are coarse nodes c * 2048 to (c + 1) * 2048 - 1 or the first 1024 nodes of column c + 1; the two entries are equal at vertices. `connect`: tetrahedra c * 4096 to (c + 1) * 4096 - 1 lie in column c; their nodes are coarse nodes of column c or the first 1024 nodes of column c + 1.
All inputs are finite; a program needn't handle non-finite values.
Results may differ from a plain program's by a relative error of at most 0.0001.
Values sent between devices are 32-bit elements; how exact they have to be, the bound alone decides.
No kernel may reach another device: no remote copies, remote signals or barrier semaphores. Data moves between devices by JAX's collectives and lax.ppermute only.
A program may use at most 64 MiB of HBM per device.

v0:
```python
import jax
import jax.numpy as jnp
from jax import lax
from jax.sharding import PartitionSpec as P

CN = 2048
CI = 1024
CE = 4096
ITERS = 3


def shifted(shard, axis, by):
    size = lax.axis_size(axis)
    pairs = [(i, i + by) for i in range(size) if 0 <= i + by < size]
    return lax.ppermute(shard, axis, pairs)


def element_forces(field, connect, grads, moduli, count):
    last = -(grads[:, 0] + grads[:, 1] + grads[:, 2])
    shape_grads = (grads[:, 0], grads[:, 1], grads[:, 2], last)
    displ_grad = jnp.zeros((3, 3, connect.shape[1]), jnp.float32)
    for corner in range(4):
        moved = jnp.take(field, connect[corner], axis=1)
        displ_grad = displ_grad + moved[:, None, :] * shape_grads[corner][None, :, :]
    strain = 0.5 * (displ_grad + jnp.transpose(displ_grad, (1, 0, 2)))
    trace = strain[0, 0] + strain[1, 1] + strain[2, 2]
    identity = jnp.eye(3, dtype=jnp.float32)[:, :, None]
    stress = 2.0 * moduli[1] * strain + moduli[0] * trace * identity
    forces = jnp.zeros((3, count), jnp.float32)
    for corner in range(4):
        nodal = jnp.sum(stress * shape_grads[corner][None, :, :], axis=1)
        forces = forces.at[:, connect[corner]].add(nodal)
    return forces


def squares(residual):
    return lax.psum(jnp.sum(residual * residual), "sub")


def body(fine_res, node_map, connect, grads, moduli, mass):
    column = lax.axis_index("sub")
    offset = column * CN
    local_map = node_map - offset
    local_conn = connect - offset
    span = CN + CI
    share = CE // lax.axis_size("grp")
    start = lax.axis_index("grp") * share
    local_conn = lax.dynamic_slice_in_dim(local_conn, start, share, 1)
    grads = lax.dynamic_slice_in_dim(grads, start, share, 2)
    moduli = lax.dynamic_slice_in_dim(moduli, start, share, 1)
    half = 0.5 * fine_res
    partial_rhs = (
        jnp.zeros((3, span), jnp.float32)
        .at[:, local_map[0]]
        .add(half)
        .at[:, local_map[1]]
        .add(half)
    )
    column_rhs = lax.psum(partial_rhs, "grp")
    carried = shifted(column_rhs[:, CN:], "sub", 1)
    rhs = column_rhs[:, :CN].at[:, :CI].add(carried)
    solution = jnp.zeros(rhs.shape, jnp.float32)
    residual = rhs
    direction = rhs
    norm_now = squares(residual)
    for step in range(ITERS):
        operate_upper = shifted(direction[:, :CI], "sub", -1)
        operate_extended = jnp.concatenate([direction, operate_upper], axis=1)
        forces = element_forces(operate_extended, local_conn, grads, moduli, span)
        forces = lax.psum(forces, "grp")
        returned = shifted(forces[:, CN:], "sub", 1)
        own = forces[:, :CN] + mass[None, :] * direction
        image = own.at[:, :CI].add(returned)
        curv = jnp.sum(direction * image)
        alpha = norm_now / lax.psum(curv, "sub")
        solution = solution + alpha * direction
        residual = residual - alpha * image
        if step + 1 < ITERS:
            norm_next = squares(residual)
            direction = residual + norm_next / norm_now * direction
            norm_now = norm_next
    upper = shifted(solution[:, :CI], "sub", -1)
    extended = jnp.concatenate([solution, upper], axis=1)
    return 0.5 * (
        jnp.take(extended, local_map[0], axis=1) + jnp.take(extended, local_map[1], axis=1)
    )


def solution(mesh):
    in_specs = (
        P(None, ("grp", "sub")),
        P(None, ("grp", "sub")),
        P(None, "sub"),
        P(None, None, "sub"),
        P(None, "sub"),
        P("sub"),
    )
    out_specs = P(None, ("grp", "sub"))
    return jax.shard_map(body, mesh=mesh, in_specs=in_specs, out_specs=out_specs, check_vma=False)
```

profile of v0, /device:TPU:0, one launch (start us, length us, event | category | flops | bytes accessed | tf_op | source)
XLA Modules:
  0.0 632.5 jit_solution(18020449593061128261)
XLA Ops:
  2.3 23.6 %scatter_custom_fusion = f32[3,3072]{0,1:T(8,128)} fusion(s32[4096]{0:T(1024)S(1)} %bitcast.139, f32[4096,3]{1,0:T(8,128)S(1)} %copy.154, f32[]{:T(128)} %constant.127.clone.1), kind=kCustom, calls=%fused_computation.56 | custom fusion | flops 12288 | bytes 36868 | tf_op jit(solution)/shard_map/scatter-add | solution.py:55
  25.9 22.7 %scatter_fusion = f32[3,3072]{0,1:T(8,128)} fusion(f32[3,3072]{0,1:T(8,128)} %scatter_custom_fusion, s32[4096]{0:T(1024)S(1)} %bitcast.112, f32[4096,3]{1,0:T(8,128)S(1)} %copy.154), kind=kCustom, calls=%fused_computation.15 | custom fusion | flops 12288 | bytes 163840 | tf_op jit(solution)/shard_map/scatter-add | solution.py:57
  48.5 34.5 %psum.70 = f32[3,3072]{0,1:T(8,128)S(1)} all-reduce(f32[3,3072]{0,1:T(8,128)} %scatter_fusion), channel_id=1, replica_groups=mesh['grp'=4,'sub'=8] {'grp'}, use_global_device_ids=true, to_apply=%region_2.0 | all-reduce | flops 9216 | bytes 73728 | tf_op jit(solution)/shard_map/psum | solution.py:59
  90.0 9.4 %collective-permute-done = f32[3,1024]{0,1:T(8,128)S(1)} collective-permute-done((f32[3,1024]{0,1:T(8,128)}, f32[3,1024]{0,1:T(8,128)S(1)}, u32[]{:S(2)}, u32[]{:S(2)}) %collective-permute-start) | collective-permute-done | bytes 12320 | tf_op jit(solution)/shard_map/ppermute | solution.py:15
  101.5 14.5 %collective-permute-done.1 = f32[3,1024]{0,1:T(8,128)S(1)} collective-permute-done((f32[3,1024]{0,1:T(8,128)S(1)}, f32[3,1024]{0,1:T(8,128)S(1)}, u32[]{:S(2)}, u32[]{:S(2)}) %collective-permute-start.1) | collective-permute-done | bytes 12320 | tf_op jit(solution)/shard_map/ppermute | solution.py:15
  139.3 6.8 %scatter_custom_fusion.2 = f32[3,3072]{0,1:T(8,128)S(1)} fusion(s32[1024]{0:T(1024)S(1)} %bitcast.140, f32[1024,3]{1,0:T(8,128)} %copy.165, f32[]{:T(128)} %constant.127.clone.1), kind=kCustom, calls=%fused_computation.54 | custom fusion | flops 3072 | bytes 37376 | tf_op jit(solution)/shard_map/scatter-add | solution.py:32
  146.1 7.0 %scatter_fusion.1 = f32[3,3072]{0,1:T(8,128)S(1)} fusion(f32[3,3072]{0,1:T(8,128)S(1)} %scatter_custom_fusion.2, s32[1024]{0:T(1024)S(1)} %bitcast.109, f32[1024,3]{1,0:T(8,128)} %copy.166), kind=kCustom, calls=%fused_computation.17 | custom fusion | flops 3072 | bytes 40960 | tf_op jit(solution)/shard_map/scatter-add | solution.py:32
  153.1 7.5 %scatter_fusion.2 = f32[3,3072]{0,1:T(8,128)S(1)} fusion(f32[3,3072]{0,1:T(8,128)S(1)} %scatter_fusion.1, s32[1024]{0:T(1024)S(1)} %bitcast.106, f32[1024,3]{1,0:T(8,128)} %copy.167), kind=kCustom, calls=%fused_computation.18 | custom fusion | flops 3072 | bytes 40960 | tf_op jit(solution)/shard_map/scatter-add | solution.py:32
  167.2 32.0 %psum.72 = f32[3,3072]{0,1:T(8,128)} all-reduce(f32[3,3072]{0,1:T(8,128)S(1)} %scatter_fusion.3), channel_id=1, replica_groups=mesh['grp'=4,'sub'=8] {'grp'}, use_global_device_ids=true, to_apply=%region_14.16 | all-reduce | flops 9216 | bytes 73728 | tf_op jit(solution)/shard_map/psum | solution.py:70
  206.2 10.0 %collective-permute-done.2 = f32[3,1024]{0,1:T(8,128)S(1)} collective-permute-done((f32[3,1024]{0,1:T(8,128)S(1)}, f32[3,1024]{0,1:T(8,128)S(1)}, u32[]{:S(2)}, u32[]{:S(2)}) %collective-permute-start.2) | collective-permute-done | bytes 12320 | tf_op jit(solution)/shard_map/ppermute | solution.py:15
  217.9 22.1 %all-reduce = (f32[]{:T(128)}, f32[]{:T(128)}) all-reduce(f32[]{:T(128)} %get-tuple-element.56, f32[]{:T(128)} %get-tuple-element.55), channel_id=1, replica_groups=mesh['grp'=4,'sub'=8] {'sub'}, use_global_device_ids=true, to_apply=%region_5.0 | all-reduce | flops 2 | bytes 16 | tf_op jit(solution)/shard_map/psum | solution.py:37
  242.3 17.9 %psum.74 = f32[]{:T(128)} all-reduce(f32[]{:T(128)} %get-tuple-element.75), channel_id=1, replica_groups=mesh['grp'=4,'sub'=8] {'sub'}, use_global_device_ids=true, to_apply=%region_18.20 | all-reduce | flops 1 | bytes 8 | tf_op jit(solution)/shard_map/psum | solution.py:37
  263.0 10.1 %collective-permute-done.3 = f32[3,1024]{0,1:T(8,128)S(1)} collective-permute-done((f32[3,1024]{0,1:T(8,128)S(1)}, f32[3,1024]{0,1:T(8,128)S(1)}, u32[]{:S(2)}, u32[]{:S(2)}) %collective-permute-start.3) | collective-permute-done | bytes 12320 | tf_op jit(solution)/shard_map/ppermute | solution.py:15
  300.0 7.4 %scatter_custom_fusion.6 = f32[3,3072]{0,1:T(8,128)} fusion(s32[1024]{0:T(1024)S(1)} %bitcast.141, f32[1024,3]{1,0:T(8,128)S(1)} %copy.177, f32[]{:T(128)} %constant.127.clone.1), kind=kCustom, calls=%fused_computation.52 | custom fusion | flops 3072 | bytes 36868 | tf_op jit(solution)/shard_map/scatter-add | solution.py:32
  308.9 8.0 %scatter_fusion.4 = f32[3,3072]{0,1:T(8,128)} fusion(f32[3,3072]{0,1:T(8,128)} %scatter_custom_fusion.6, s32[1024]{0:T(1024)S(1)} %bitcast.110, f32[1024,3]{1,0:T(8,128)S(1)} %copy.178), kind=kCustom, calls=%fused_computation.21 | custom fusion | flops 3072 | bytes 40960 | tf_op jit(solution)/shard_map/scatter-add | solution.py:32
  316.9 8.0 %scatter_fusion.5 = f32[3,3072]{0,1:T(8,128)} fusion(f32[3,3072]{0,1:T(8,128)} %scatter_fusion.4, s32[1024]{0:T(1024)S(1)} %bitcast.107, f32[1024,3]{1,0:T(8,128)S(1)} %copy.179), kind=kCustom, calls=%fused_computation.22 | custom fusion | flops 3072 | bytes 40960 | tf_op jit(solution)/shard_map/scatter-add | solution.py:32
  324.8 8.4 %scatter_fusion.6 = f32[3,3072]{0,1:T(8,128)} fusion(f32[3,3072]{0,1:T(8,128)} %scatter_fusion.5, s32[1024]{0:T(1024)S(1)} %bitcast.104, f32[1024,3]{1,0:T(8,128)} %copy.180), kind=kCustom, calls=%fused_computation.23 | custom fusion | flops 3072 | bytes 40960 | tf_op jit(solution)/shard_map/scatter-add | solution.py:32
  333.2 32.8 %psum.75 = f32[3,3072]{0,1:T(8,128)} all-reduce(f32[3,3072]{0,1:T(8,128)} %scatter_fusion.6), channel_id=1, replica_groups=mesh['grp'=4,'sub'=8] {'grp'}, use_global_device_ids=true, to_apply=%region_27.29 | all-reduce | flops 9216 | bytes 73728 | tf_op jit(solution)/shard_map/psum | solution.py:70
  373.5 10.0 %collective-permute-done.4 = f32[3,1024]{0,1:T(8,128)S(1)} collective-permute-done((f32[3,1024]{0,1:T(8,128)S(1)}, f32[3,1024]{0,1:T(8,128)S(1)}, u32[]{:S(2)}, u32[]{:S(2)}) %collective-permute-start.4) | collective-permute-done | bytes 12320 | tf_op jit(solution)/shard_map/ppermute | solution.py:15
  385.2 20.3 %psum.76 = f32[]{:T(128)} all-reduce(f32[]{:T(128)} %multiply_reduce_fusion.2), channel_id=1, replica_groups=mesh['grp'=4,'sub'=8] {'sub'}, use_global_device_ids=true, to_apply=%region_29.31 | all-reduce | flops 1 | bytes 8 | tf_op jit(solution)/shard_map/psum | solution.py:75
  409.0 17.7 %psum.77 = f32[]{:T(128)} all-reduce(f32[]{:T(128)} %multiply_reduce_fusion.1), channel_id=1, replica_groups=mesh['grp'=4,'sub'=8] {'sub'}, use_global_device_ids=true, to_apply=%region_31.33 | all-reduce | flops 1 | bytes 8 | tf_op jit(solution)/shard_map/psum | solution.py:37
  431.2 9.5 %collective-permute-done.5 = f32[3,1024]{0,1:T(8,128)S(1)} collective-permute-done((f32[3,1024]{0,1:T(8,128)S(1)}, f32[3,1024]{0,1:T(8,128)S(1)}, u32[]{:S(2)}, u32[]{:S(2)}) %collective-permute-start.5) | collective-permute-done | bytes 12320 | tf_op jit(solution)/shard_map/ppermute | solution.py:15
  478.1 7.6 %scatter_custom_fusion.10 = f32[3,3072]{0,1:T(8,128)} fusion(s32[1024]{0:T(1024)S(1)} %bitcast.142, f32[1024,3]{1,0:T(8,128)} %copy.189, f32[]{:T(128)} %constant.127.clone.1), kind=kCustom, calls=%fused_computation.50 | custom fusion | flops 3072 | bytes 37376 | tf_op jit(solution)/shard_map/scatter-add | solution.py:32
  488.8 8.4 %scatter_fusion.7 = f32[3,3072]{0,1:T(8,128)} fusion(f32[3,3072]{0,1:T(8,128)} %scatter_custom_fusion.10, s32[1024]{0:T(1024)S(1)} %bitcast.111, f32[1024,3]{1,0:T(8,128)} %copy.190), kind=kCustom, calls=%fused_computation.25 | custom fusion | flops 3072 | bytes 40960 | tf_op jit(solution)/shard_map/scatter-add | solution.py:32
  497.2 8.4 %scatter_fusion.8 = f32[3,3072]{0,1:T(8,128)} fusion(f32[3,3072]{0,1:T(8,128)} %scatter_fusion.7, s32[1024]{0:T(1024)S(1)} %bitcast.108, f32[1024,3]{1,0:T(8,128)} %copy.191), kind=kCustom, calls=%fused_computation.26 | custom fusion | flops 3072 | bytes 40960 | tf_op jit(solution)/shard_map/scatter-add | solution.py:32
  505.5 8.4 %scatter_fusion.9 = f32[3,3072]{0,1:T(8,128)} fusion(f32[3,3072]{0,1:T(8,128)} %scatter_fusion.8, s32[1024]{0:T(1024)S(1)} %bitcast.105, f32[1024,3]{1,0:T(8,128)} %copy.192), kind=kCustom, calls=%fused_computation.27 | custom fusion | flops 3072 | bytes 40960 | tf_op jit(solution)/shard_map/scatter-add | solution.py:32
  513.9 32.9 %psum.78 = f32[3,3072]{0,1:T(8,128)} all-reduce(f32[3,3072]{0,1:T(8,128)} %scatter_fusion.9), channel_id=1, replica_groups=mesh['grp'=4,'sub'=8] {'grp'}, use_global_device_ids=true, to_apply=%region_40.42 | all-reduce | flops 9216 | bytes 73728 | tf_op jit(solution)/shard_map/psum | solution.py:70
  554.3 9.9 %collective-permute-done.6 = f32[3,1024]{0,1:T(8,128)S(1)} collective-permute-done((f32[3,1024]{0,1:T(8,128)S(1)}, f32[3,1024]{0,1:T(8,128)S(1)}, u32[]{:S(2)}, u32[]{:S(2)}) %collective-permute-start.6) | collective-permute-done | bytes 12320 | tf_op jit(solution)/shard_map/ppermute | solution.py:15
  565.9 20.2 %psum.79 = f32[]{:T(128)} all-reduce(f32[]{:T(128)} %multiply_reduce_fusion), channel_id=1, replica_groups=mesh['grp'=4,'sub'=8] {'sub'}, use_global_device_ids=true, to_apply=%region_42.44 | all-reduce | flops 1 | bytes 8 | tf_op jit(solution)/shard_map/psum | solution.py:75
  588.9 9.9 %collective-permute-done.7 = f32[3,1024]{0,1:T(8,128)S(1)} collective-permute-done((f32[3,1024]{0,1:T(8,128)S(1)}, f32[3,1024]{0,1:T(8,128)S(1)}, u32[]{:S(2)}, u32[]{:S(2)}) %collective-permute-start.7) | collective-permute-done | bytes 12320 | tf_op jit(solution)/shard_map/ppermute | solution.py:15
  599.0 14.1 %gather_fusion.12 = f32[4096,3]{1,0:T(8,128)} fusion(f32[3,3072]{0,1:T(8,128)S(1)} %pad_maximum_fusion.3, s32[4096]{0:T(1024)S(1)} %fusion.12), kind=kCustom, calls=%fused_computation.1.clone | custom fusion | bytes 114688 | tf_op jit(solution)/shard_map/jit(_take)/gather | solution.py:85
  615.3 14.1 %gather_fusion.13 = f32[4096,3]{1,0:T(8,128)} fusion(f32[3,3072]{0,1:T(8,128)S(1)} %pad_maximum_fusion.3, s32[4096]{0:T(1024)S(1)} %fusion.13), kind=kCustom, calls=%fused_computation.13.clone | custom fusion | bytes 114688 | tf_op jit(solution)/shard_map/jit(_take)/gather | solution.py:85
  (126 shorter events, 151.4 us)
Async XLA Ops:
  83.9 15.5 %collective-permute-start = (f32[3,1024]{0,1:T(8,128)}, f32[3,1024]{0,1:T(8,128)S(1)}, u32[]{:S(2)}, u32[]{:S(2)}) collective-permute-start(f32[3,1024]{0,1:T(8,128)} %slice.282), channel_id=1, source_target_pairs={{0,1},{1,2},{2,3},{3,4},{4,5},{5,6},{6,7},{8,9},{9,10},{10,11},{11... | collective-permute-start | bytes 36872 | tf_op jit(solution)/shard_map/ppermute | solution.py:15
  89.3 12.1 %copy-start.3 = (f32[2,4096]{1,0:T(2,128)S(1)}, f32[2,4096]{1,0:T(2,128)}, u32[]{:S(2)}) copy-start(f32[2,4096]{1,0:T(2,128)} %param.22) | copy-start | bytes 98308
  100.1 15.9 %collective-permute-start.1 = (f32[3,1024]{0,1:T(8,128)S(1)}, f32[3,1024]{0,1:T(8,128)S(1)}, u32[]{:S(2)}, u32[]{:S(2)}) collective-permute-start(f32[3,1024]{0,1:T(8,128)S(1)} %get-tuple-element.80), channel_id=1, source_target_pairs={{1,0},{2,1},{3,2},{4,3},{5,4},{6,5},{7,6},{9,8},{10,9},{11,10},{12... | collective-permute-start | bytes 36872 | tf_op jit(solution)/shard_map/ppermute | solution.py:15
  167.2 37.4 %copy-start.2 = (f32[2048]{0:T(1024)S(1)}, f32[2048]{0:T(1024)}, u32[]{:S(2)}) copy-start(f32[2048]{0:T(1024)} %param.23) | copy-start | bytes 24580
  200.3 15.9 %collective-permute-start.2 = (f32[3,1024]{0,1:T(8,128)S(1)}, f32[3,1024]{0,1:T(8,128)S(1)}, u32[]{:S(2)}, u32[]{:S(2)}) collective-permute-start(f32[3,1024]{0,1:T(8,128)S(1)} %slice.292), channel_id=1, source_target_pairs={{0,1},{1,2},{2,3},{3,4},{4,5},{5,6},{6,7},{8,9},{9,10},{10,11},{11... | collective-permute-start | bytes 36872 | tf_op jit(solution)/shard_map/ppermute | solution.py:15
  242.3 19.3 %copy-start.1 = (f32[3,2048]{0,1:T(8,128)}, f32[3,2048]{0,1:T(8,128)S(1)}, u32[]{:S(2)}) copy-start(f32[3,2048]{0,1:T(8,128)S(1)} %get-tuple-element.76) | copy-start | bytes 73732
  261.7 11.4 %collective-permute-start.3 = (f32[3,1024]{0,1:T(8,128)S(1)}, f32[3,1024]{0,1:T(8,128)S(1)}, u32[]{:S(2)}, u32[]{:S(2)}) collective-permute-start(f32[3,1024]{0,1:T(8,128)S(1)} %slice.293), channel_id=1, source_target_pairs={{1,0},{2,1},{3,2},{4,3},{5,4},{6,5},{7,6},{9,8},{10,9},{11,10},{12... | collective-permute-start | bytes 36872 | tf_op jit(solution)/shard_map/ppermute | solution.py:15
  367.0 16.4 %collective-permute-start.4 = (f32[3,1024]{0,1:T(8,128)S(1)}, f32[3,1024]{0,1:T(8,128)S(1)}, u32[]{:S(2)}, u32[]{:S(2)}) collective-permute-start(f32[3,1024]{0,1:T(8,128)S(1)} %slice.299), channel_id=1, source_target_pairs={{0,1},{1,2},{2,3},{3,4},{4,5},{5,6},{6,7},{8,9},{9,10},{10,11},{11... | collective-permute-start | bytes 36872 | tf_op jit(solution)/shard_map/ppermute | solution.py:15
  384.2 24.7 %copy-start = (f32[3,2048]{0,1:T(8,128)}, f32[3,2048]{0,1:T(8,128)S(1)}, u32[]{:S(2)}) copy-start(f32[3,2048]{0,1:T(8,128)S(1)} %fusion.9) | copy-start | bytes 73732
  429.7 11.1 %collective-permute-start.5 = (f32[3,1024]{0,1:T(8,128)S(1)}, f32[3,1024]{0,1:T(8,128)S(1)}, u32[]{:S(2)}, u32[]{:S(2)}) collective-permute-start(f32[3,1024]{0,1:T(8,128)S(1)} %slice.300), channel_id=1, source_target_pairs={{1,0},{2,1},{3,2},{4,3},{5,4},{6,5},{7,6},{9,8},{10,9},{11,10},{12... | collective-permute-start | bytes 36872 | tf_op jit(solution)/shard_map/ppermute | solution.py:15
  547.9 16.3 %collective-permute-start.6 = (f32[3,1024]{0,1:T(8,128)S(1)}, f32[3,1024]{0,1:T(8,128)S(1)}, u32[]{:S(2)}, u32[]{:S(2)}) collective-permute-start(f32[3,1024]{0,1:T(8,128)S(1)} %slice.306), channel_id=1, source_target_pairs={{0,1},{1,2},{2,3},{3,4},{4,5},{5,6},{6,7},{8,9},{9,10},{10,11},{11... | collective-permute-start | bytes 36872 | tf_op jit(solution)/shard_map/ppermute | solution.py:15
  587.6 11.3 %collective-permute-start.7 = (f32[3,1024]{0,1:T(8,128)S(1)}, f32[3,1024]{0,1:T(8,128)S(1)}, u32[]{:S(2)}, u32[]{:S(2)}) collective-permute-start(f32[3,1024]{0,1:T(8,128)S(1)} %slice.307), channel_id=1, source_target_pairs={{1,0},{2,1},{3,2},{4,3},{5,4},{6,5},{7,6},{9,8},{10,9},{11,10},{12... | collective-permute-start | bytes 36872 | tf_op jit(solution)/shard_map/ppermute | solution.py:15
where the time goes:
time: 643 us; the launch traced here: 632 us
  blocking collectives  230 us (36%)
  other arithmetic  178 us (28%)
  local copies, waits for them, and re-layouts  111 us (17%)
  waiting for transfers between devices  83.3 us (13%)
  starting transfers between devices  22.8 us (4%)
  between operations  7.44 us (1%)
    psum x3, blocking collectives, body(): forces = lax.psum(forces, 'grp')  97.6 us
    scatter-add x12, other arithmetic, element_forces(): forces = forces.at[:, connect[corner]].add(nodal)  92.3 us
    ppermute x8, waiting for transfers between devices, shifted(): return lax.ppermute(shard, axis, pairs)  83.3 us
    psum x3, blocking collectives, squares(): return lax.psum(jnp.sum(residual * residual), 'sub')  57.7 us
    gather x12, local copies, waits for them, and re-layouts, element_forces(): moved = jnp.take(field, connect[corner], axis=1)  56.8 us
    scatter-add x2, other arithmetic, body(): partial_rhs = jnp.zeros((3, span), jnp.float32).at[:, local_map[0]].add(h...  46.2 us
    psum x2, blocking collectives, body(): alpha = norm_now / lax.psum(curv, 'sub')  40.5 us
    psum x1, blocking collectives, body(): column_rhs = lax.psum(partial_rhs, 'grp')  34.5 us
  transfers between devices with their start and end apart: 8, of which 8 were waited for; matrix products, arithmetic and copies ran while one was open for 1% of the time, Pallas kernels for 0%

commit v1 on v0

--- a/solution.py
+++ b/solution.py
@@ -56,7 +56,7 @@
         .at[:, local_map[1]]
         .add(half)
     )
-    column_rhs = lax.psum(partial_rhs, "grp")
+    column_rhs = jnp.sum(jax.lax.all_gather(partial_rhs, "grp"), axis=0)
     carried = shifted(column_rhs[:, CN:], "sub", 1)
     rhs = column_rhs[:, :CN].at[:, :CI].add(carried)
     solution = jnp.zeros(rhs.shape, jnp.float32)

time: 643 us -> 617 us (0.960)
  blocking collectives: 230 us -> 203 us
    psum x1 -> x0, blocking collectives: 34.5 us -> none  [body(): column_rhs = lax.psum(partial_rhs, 'grp')]
    all_gather x0 -> x1, blocking collectives: none -> 6.86 us  [body(): column_rhs = jnp.sum(jax.lax.all_gather(partial_rhs, 'grp'), axis=0)]
where the time goes in v1:
time: 617 us; the launch traced here: 607 us
  blocking collectives  203 us (33%)
  other arithmetic  178 us (29%)
  local copies, waits for them, and re-layouts  113 us (18%)
  waiting for transfers between devices  83.2 us (13%)
  starting transfers between devices  23.2 us (4%)
  between operations  7.47 us (1%)
    psum x3, blocking collectives, body(): forces = lax.psum(forces, 'grp')  97.8 us
    scatter-add x12, other arithmetic, element_forces(): forces = forces.at[:, connect[corner]].add(nodal)  92.3 us
    ppermute x8, waiting for transfers between devices, shifted(): return lax.ppermute(shard, axis, pairs)  83.2 us
    psum x3, blocking collectives, squares(): return lax.psum(jnp.sum(residual * residual), 'sub')  57.6 us
    gather x12, local copies, waits for them, and re-layouts, element_forces(): moved = jnp.take(field, connect[corner], axis=1)  56.8 us
    scatter-add x2, other arithmetic, body(): partial_rhs = jnp.zeros((3, span), jnp.float32).at[:, local_map[0]].add(h...  46.3 us
    psum x2, blocking collectives, body(): alpha = norm_now / lax.psum(curv, 'sub')  40.5 us
    ppermute x8, starting transfers between devices, shifted(): return lax.ppermute(shard, axis, pairs)  23.2 us
  transfers between devices with their start and end apart: 8, of which 8 were waited for; matrix products, arithmetic and copies ran while one was open for 1% of the time, Pallas kernels for 0%

profile of v1, /device:TPU:0, one launch (start us, length us, event | category | flops | bytes accessed | tf_op | source)
XLA Modules:
  0.0 607.3 jit_solution(5054294759038939380)
XLA Ops:
  3.7 23.0 %scatter_custom_fusion = f32[3,3072]{0,1:T(8,128)S(1)} fusion(s32[4096]{0:T(1024)S(1)} %bitcast.141, f32[4096,3]{1,0:T(8,128)} %copy.215, f32[]{:T(128)} %constant.127.clone.1), kind=kCustom, calls=%fused_computation.56 | custom fusion | flops 12288 | bytes 37376 | tf_op jit(solution)/shard_map/scatter-add | solution.py:55
  26.7 23.3 %scatter_fusion = f32[3,3072]{0,1:T(8,128)S(1)} fusion(f32[3,3072]{0,1:T(8,128)S(1)} %scatter_custom_fusion, s32[4096]{0:T(1024)S(1)} %bitcast.114, f32[4096,3]{1,0:T(8,128)} %copy.215), kind=kCustom, calls=%fused_computation.15 | custom fusion | flops 12288 | bytes 163840 | tf_op jit(solution)/shard_map/scatter-add | solution.py:57
  50.5 6.9 %all-gather.1 = f32[4,3,3072]{2,1,0:T(4,128)S(1)} all-gather(f32[1,3,3072]{2,1,0:T(4,128)S(1)} %copy.217), channel_id=2, replica_groups=mesh['grp'=4,'sub'=8] {'grp'}, dimensions={0}, use_global_device_ids=true | all-gather | bytes 184320 | tf_op jit(solution)/shard_map/all_gather | solution.py:59
  64.5 8.5 %collective-permute-done = f32[3,1024]{0,1:T(8,128)S(1)} collective-permute-done((f32[3,1024]{0,1:T(8,128)S(1)}, f32[3,1024]{0,1:T(8,128)S(1)}, u32[]{:S(2)}, u32[]{:S(2)}) %collective-permute-start) | collective-permute-done | bytes 12320 | tf_op jit(solution)/shard_map/ppermute | solution.py:15
  75.1 14.5 %collective-permute-done.1 = f32[3,1024]{0,1:T(8,128)S(1)} collective-permute-done((f32[3,1024]{0,1:T(8,128)S(1)}, f32[3,1024]{0,1:T(8,128)S(1)}, u32[]{:S(2)}, u32[]{:S(2)}) %collective-permute-start.1) | collective-permute-done | bytes 12320 | tf_op jit(solution)/shard_map/ppermute | solution.py:15
  112.9 6.8 %scatter_custom_fusion.2 = f32[3,3072]{0,1:T(8,128)S(1)} fusion(s32[1024]{0:T(1024)S(1)} %bitcast.142, f32[1024,3]{1,0:T(8,128)} %copy.231, f32[]{:T(128)} %constant.127.clone.1), kind=kCustom, calls=%fused_computation.54 | custom fusion | flops 3072 | bytes 37376 | tf_op jit(solution)/shard_map/scatter-add | solution.py:32
  119.7 7.5 %scatter_fusion.1 = f32[3,3072]{0,1:T(8,128)S(1)} fusion(f32[3,3072]{0,1:T(8,128)S(1)} %scatter_custom_fusion.2, s32[1024]{0:T(1024)S(1)} %bitcast.111, f32[1024,3]{1,0:T(8,128)} %copy.232), kind=kCustom, calls=%fused_computation.17 | custom fusion | flops 3072 | bytes 40960 | tf_op jit(solution)/shard_map/scatter-add | solution.py:32
  127.2 7.0 %scatter_fusion.2 = f32[3,3072]{0,1:T(8,128)S(1)} fusion(f32[3,3072]{0,1:T(8,128)S(1)} %scatter_fusion.1, s32[1024]{0:T(1024)S(1)} %bitcast.108, f32[1024,3]{1,0:T(8,128)} %copy.233), kind=kCustom, calls=%fused_computation.18 | custom fusion | flops 3072 | bytes 40960 | tf_op jit(solution)/shard_map/scatter-add | solution.py:32
  140.9 32.6 %psum.64 = f32[3,3072]{0,1:T(8,128)} all-reduce(f32[3,3072]{0,1:T(8,128)S(1)} %scatter_fusion.3), channel_id=1, replica_groups=mesh['grp'=4,'sub'=8] {'grp'}, use_global_device_ids=true, to_apply=%region_14.16 | all-reduce | flops 9216 | bytes 73728 | tf_op jit(solution)/shard_map/psum | solution.py:70
  180.7 9.8 %collective-permute-done.2 = f32[3,1024]{0,1:T(8,128)S(1)} collective-permute-done((f32[3,1024]{0,1:T(8,128)S(1)}, f32[3,1024]{0,1:T(8,128)S(1)}, u32[]{:S(2)}, u32[]{:S(2)}) %collective-permute-start.2) | collective-permute-done | bytes 12320 | tf_op jit(solution)/shard_map/ppermute | solution.py:15
  192.2 22.1 %all-reduce = (f32[]{:T(128)}, f32[]{:T(128)}) all-reduce(f32[]{:T(128)} %get-tuple-element.56, f32[]{:T(128)} %get-tuple-element.55), channel_id=1, replica_groups=mesh['grp'=4,'sub'=8] {'sub'}, use_global_device_ids=true, to_apply=%region_5.0 | all-reduce | flops 2 | bytes 16 | tf_op jit(solution)/shard_map/psum | solution.py:37
  216.6 17.9 %psum.66 = f32[]{:T(128)} all-reduce(f32[]{:T(128)} %get-tuple-element.75), channel_id=1, replica_groups=mesh['grp'=4,'sub'=8] {'sub'}, use_global_device_ids=true, to_apply=%region_18.20 | all-reduce | flops 1 | bytes 8 | tf_op jit(solution)/shard_map/psum | solution.py:37
  237.3 10.1 %collective-permute-done.3 = f32[3,1024]{0,1:T(8,128)S(1)} collective-permute-done((f32[3,1024]{0,1:T(8,128)S(1)}, f32[3,1024]{0,1:T(8,128)S(1)}, u32[]{:S(2)}, u32[]{:S(2)}) %collective-permute-start.3) | collective-permute-done | bytes 12320 | tf_op jit(solution)/shard_map/ppermute | solution.py:15
  274.3 7.4 %scatter_custom_fusion.6 = f32[3,3072]{0,1:T(8,128)} fusion(s32[1024]{0:T(1024)S(1)} %bitcast.143, f32[1024,3]{1,0:T(8,128)S(1)} %copy.243, f32[]{:T(128)} %constant.127.clone.1), kind=kCustom, calls=%fused_computation.52 | custom fusion | flops 3072 | bytes 36868 | tf_op jit(solution)/shard_map/scatter-add | solution.py:32
  283.2 8.0 %scatter_fusion.4 = f32[3,3072]{0,1:T(8,128)} fusion(f32[3,3072]{0,1:T(8,128)} %scatter_custom_fusion.6, s32[1024]{0:T(1024)S(1)} %bitcast.112, f32[1024,3]{1,0:T(8,128)S(1)} %copy.244), kind=kCustom, calls=%fused_computation.21 | custom fusion | flops 3072 | bytes 40960 | tf_op jit(solution)/shard_map/scatter-add | solution.py:32
  291.1 8.0 %scatter_fusion.5 = f32[3,3072]{0,1:T(8,128)} fusion(f32[3,3072]{0,1:T(8,128)} %scatter_fusion.4, s32[1024]{0:T(1024)S(1)} %bitcast.109, f32[1024,3]{1,0:T(8,128)S(1)} %copy.245), kind=kCustom, calls=%fused_computation.22 | custom fusion | flops 3072 | bytes 40960 | tf_op jit(solution)/shard_map/scatter-add | solution.py:32
  299.1 8.4 %scatter_fusion.6 = f32[3,3072]{0,1:T(8,128)} fusion(f32[3,3072]{0,1:T(8,128)} %scatter_fusion.5, s32[1024]{0:T(1024)S(1)} %bitcast.106, f32[1024,3]{1,0:T(8,128)} %copy.246), kind=kCustom, calls=%fused_computation.23 | custom fusion | flops 3072 | bytes 40960 | tf_op jit(solution)/shard_map/scatter-add | solution.py:32
  307.5 32.5 %psum.67 = f32[3,3072]{0,1:T(8,128)} all-reduce(f32[3,3072]{0,1:T(8,128)} %scatter_fusion.6), channel_id=1, replica_groups=mesh['grp'=4,'sub'=8] {'grp'}, use_global_device_ids=true, to_apply=%region_27.29 | all-reduce | flops 9216 | bytes 73728 | tf_op jit(solution)/shard_map/psum | solution.py:70
  347.5 10.2 %collective-permute-done.4 = f32[3,1024]{0,1:T(8,128)S(1)} collective-permute-done((f32[3,1024]{0,1:T(8,128)S(1)}, f32[3,1024]{0,1:T(8,128)S(1)}, u32[]{:S(2)}, u32[]{:S(2)}) %collective-permute-start.4) | collective-permute-done | bytes 12320 | tf_op jit(solution)/shard_map/ppermute | solution.py:15
  359.5 20.3 %psum.68 = f32[]{:T(128)} all-reduce(f32[]{:T(128)} %multiply_reduce_fusion.2), channel_id=1, replica_groups=mesh['grp'=4,'sub'=8] {'sub'}, use_global_device_ids=true, to_apply=%region_29.31 | all-reduce | flops 1 | bytes 8 | tf_op jit(solution)/shard_map/psum | solution.py:75
  383.3 17.7 %psum.69 = f32[]{:T(128)} all-reduce(f32[]{:T(128)} %multiply_reduce_fusion.1), channel_id=1, replica_groups=mesh['grp'=4,'sub'=8] {'sub'}, use_global_device_ids=true, to_apply=%region_31.33 | all-reduce | flops 1 | bytes 8 | tf_op jit(solution)/shard_map/psum | solution.py:37
  405.5 9.5 %collective-permute-done.5 = f32[3,1024]{0,1:T(8,128)S(1)} collective-permute-done((f32[3,1024]{0,1:T(8,128)S(1)}, f32[3,1024]{0,1:T(8,128)S(1)}, u32[]{:S(2)}, u32[]{:S(2)}) %collective-permute-start.5) | collective-permute-done | bytes 12320 | tf_op jit(solution)/shard_map/ppermute | solution.py:15
  452.3 7.6 %scatter_custom_fusion.10 = f32[3,3072]{0,1:T(8,128)} fusion(s32[1024]{0:T(1024)S(1)} %bitcast.144, f32[1024,3]{1,0:T(8,128)} %copy.255, f32[]{:T(128)} %constant.127.clone.1), kind=kCustom, calls=%fused_computation.50 | custom fusion | flops 3072 | bytes 37376 | tf_op jit(solution)/shard_map/scatter-add | solution.py:32
  463.1 8.4 %scatter_fusion.7 = f32[3,3072]{0,1:T(8,128)} fusion(f32[3,3072]{0,1:T(8,128)} %scatter_custom_fusion.10, s32[1024]{0:T(1024)S(1)} %bitcast.113, f32[1024,3]{1,0:T(8,128)} %copy.256), kind=kCustom, calls=%fused_computation.25 | custom fusion | flops 3072 | bytes 40960 | tf_op jit(solution)/shard_map/scatter-add | solution.py:32
  471.4 8.4 %scatter_fusion.8 = f32[3,3072]{0,1:T(8,128)} fusion(f32[3,3072]{0,1:T(8,128)} %scatter_fusion.7, s32[1024]{0:T(1024)S(1)} %bitcast.110, f32[1024,3]{1,0:T(8,128)} %copy.257), kind=kCustom, calls=%fused_computation.26 | custom fusion | flops 3072 | bytes 40960 | tf_op jit(solution)/shard_map/scatter-add | solution.py:32
  479.8 8.4 %scatter_fusion.9 = f32[3,3072]{0,1:T(8,128)} fusion(f32[3,3072]{0,1:T(8,128)} %scatter_fusion.8, s32[1024]{0:T(1024)S(1)} %bitcast.107, f32[1024,3]{1,0:T(8,128)} %copy.258), kind=kCustom, calls=%fused_computation.27 | custom fusion | flops 3072 | bytes 40960 | tf_op jit(solution)/shard_map/scatter-add | solution.py:32
  488.2 32.7 %psum.70 = f32[3,3072]{0,1:T(8,128)} all-reduce(f32[3,3072]{0,1:T(8,128)} %scatter_fusion.9), channel_id=1, replica_groups=mesh['grp'=4,'sub'=8] {'grp'}, use_global_device_ids=true, to_apply=%region_40.42 | all-reduce | flops 9216 | bytes 73728 | tf_op jit(solution)/shard_map/psum | solution.py:70
  528.3 10.1 %collective-permute-done.6 = f32[3,1024]{0,1:T(8,128)S(1)} collective-permute-done((f32[3,1024]{0,1:T(8,128)S(1)}, f32[3,1024]{0,1:T(8,128)S(1)}, u32[]{:S(2)}, u32[]{:S(2)}) %collective-permute-start.6) | collective-permute-done | bytes 12320 | tf_op jit(solution)/shard_map/ppermute | solution.py:15
  540.1 20.2 %psum.71 = f32[]{:T(128)} all-reduce(f32[]{:T(128)} %multiply_reduce_fusion), channel_id=1, replica_groups=mesh['grp'=4,'sub'=8] {'sub'}, use_global_device_ids=true, to_apply=%region_42.44 | all-reduce | flops 1 | bytes 8 | tf_op jit(solution)/shard_map/psum | solution.py:75
  563.2 10.5 %collective-permute-done.7 = f32[3,1024]{0,1:T(8,128)S(1)} collective-permute-done((f32[3,1024]{0,1:T(8,128)S(1)}, f32[3,1024]{0,1:T(8,128)S(1)}, u32[]{:S(2)}, u32[]{:S(2)}) %collective-permute-start.7) | collective-permute-done | bytes 12320 | tf_op jit(solution)/shard_map/ppermute | solution.py:15
  573.8 14.1 %gather_fusion.12 = f32[4096,3]{1,0:T(8,128)} fusion(f32[3,3072]{0,1:T(8,128)S(1)} %pad_maximum_fusion.3, s32[4096]{0:T(1024)S(1)} %fusion.12), kind=kCustom, calls=%fused_computation.1.clone | custom fusion | bytes 114688 | tf_op jit(solution)/shard_map/jit(_take)/gather | solution.py:85
  590.0 14.1 %gather_fusion.13 = f32[4096,3]{1,0:T(8,128)} fusion(f32[3,3072]{0,1:T(8,128)S(1)} %pad_maximum_fusion.3, s32[4096]{0:T(1024)S(1)} %fusion.13), kind=kCustom, calls=%fused_computation.13.clone | custom fusion | bytes 114688 | tf_op jit(solution)/shard_map/jit(_take)/gather | solution.py:85
  (131 shorter events, 153.6 us)
Async XLA Ops:
  57.6 15.3 %collective-permute-start = (f32[3,1024]{0,1:T(8,128)S(1)}, f32[3,1024]{0,1:T(8,128)S(1)}, u32[]{:S(2)}, u32[]{:S(2)}) collective-permute-start(f32[3,1024]{0,1:T(8,128)S(1)} %copy.218), channel_id=1, source_target_pairs={{0,1},{1,2},{2,3},{3,4},{4,5},{5,6},{6,7},{8,9},{9,10},{10,11},{11... | collective-permute-start | bytes 36872 | tf_op jit(solution)/shard_map/ppermute | solution.py:15
  63.5 11.5 %copy-start.3 = (f32[2,4096]{1,0:T(2,128)S(1)}, f32[2,4096]{1,0:T(2,128)}, u32[]{:S(2)}) copy-start(f32[2,4096]{1,0:T(2,128)} %param.22) | copy-start | bytes 98308
  73.7 16.0 %collective-permute-start.1 = (f32[3,1024]{0,1:T(8,128)S(1)}, f32[3,1024]{0,1:T(8,128)S(1)}, u32[]{:S(2)}, u32[]{:S(2)}) collective-permute-start(f32[3,1024]{0,1:T(8,128)S(1)} %get-tuple-element.80), channel_id=1, source_target_pairs={{1,0},{2,1},{3,2},{4,3},{5,4},{6,5},{7,6},{9,8},{10,9},{11,10},{12... | collective-permute-start | bytes 36872 | tf_op jit(solution)/shard_map/ppermute | solution.py:15
  140.9 38.2 %copy-start.2 = (f32[2048]{0:T(1024)S(1)}, f32[2048]{0:T(1024)}, u32[]{:S(2)}) copy-start(f32[2048]{0:T(1024)} %param.23) | copy-start | bytes 24580
  174.5 16.0 %collective-permute-start.2 = (f32[3,1024]{0,1:T(8,128)S(1)}, f32[3,1024]{0,1:T(8,128)S(1)}, u32[]{:S(2)}, u32[]{:S(2)}) collective-permute-start(f32[3,1024]{0,1:T(8,128)S(1)} %slice.292), channel_id=1, source_target_pairs={{0,1},{1,2},{2,3},{3,4},{4,5},{5,6},{6,7},{8,9},{9,10},{10,11},{11... | collective-permute-start | bytes 36872 | tf_op jit(solution)/shard_map/ppermute | solution.py:15
  216.6 19.3 %copy-start.1 = (f32[3,2048]{0,1:T(8,128)}, f32[3,2048]{0,1:T(8,128)S(1)}, u32[]{:S(2)}) copy-start(f32[3,2048]{0,1:T(8,128)S(1)} %get-tuple-element.76) | copy-start | bytes 73732
  236.0 11.4 %collective-permute-start.3 = (f32[3,1024]{0,1:T(8,128)S(1)}, f32[3,1024]{0,1:T(8,128)S(1)}, u32[]{:S(2)}, u32[]{:S(2)}) collective-permute-start(f32[3,1024]{0,1:T(8,128)S(1)} %slice.293), channel_id=1, source_target_pairs={{1,0},{2,1},{3,2},{4,3},{5,4},{6,5},{7,6},{9,8},{10,9},{11,10},{12... | collective-permute-start | bytes 36872 | tf_op jit(solution)/shard_map/ppermute | solution.py:15
  341.1 16.6 %collective-permute-start.4 = (f32[3,1024]{0,1:T(8,128)S(1)}, f32[3,1024]{0,1:T(8,128)S(1)}, u32[]{:S(2)}, u32[]{:S(2)}) collective-permute-start(f32[3,1024]{0,1:T(8,128)S(1)} %slice.299), channel_id=1, source_target_pairs={{0,1},{1,2},{2,3},{3,4},{4,5},{5,6},{6,7},{8,9},{9,10},{10,11},{11... | collective-permute-start | bytes 36872 | tf_op jit(solution)/shard_map/ppermute | solution.py:15
  358.5 24.7 %copy-start = (f32[3,2048]{0,1:T(8,128)}, f32[3,2048]{0,1:T(8,128)S(1)}, u32[]{:S(2)}) copy-start(f32[3,2048]{0,1:T(8,128)S(1)} %fusion.9) | copy-start | bytes 73732
  403.9 11.1 %collective-permute-start.5 = (f32[3,1024]{0,1:T(8,128)S(1)}, f32[3,1024]{0,1:T(8,128)S(1)}, u32[]{:S(2)}, u32[]{:S(2)}) collective-permute-start(f32[3,1024]{0,1:T(8,128)S(1)} %slice.300), channel_id=1, source_target_pairs={{1,0},{2,1},{3,2},{4,3},{5,4},{6,5},{7,6},{9,8},{10,9},{11,10},{12... | collective-permute-start | bytes 36872 | tf_op jit(solution)/shard_map/ppermute | solution.py:15
  521.9 16.4 %collective-permute-start.6 = (f32[3,1024]{0,1:T(8,128)S(1)}, f32[3,1024]{0,1:T(8,128)S(1)}, u32[]{:S(2)}, u32[]{:S(2)}) collective-permute-start(f32[3,1024]{0,1:T(8,128)S(1)} %slice.306), channel_id=1, source_target_pairs={{0,1},{1,2},{2,3},{3,4},{4,5},{5,6},{6,7},{8,9},{9,10},{10,11},{11... | collective-permute-start | bytes 36872 | tf_op jit(solution)/shard_map/ppermute | solution.py:15
  561.8 11.8 %collective-permute-start.7 = (f32[3,1024]{0,1:T(8,128)S(1)}, f32[3,1024]{0,1:T(8,128)S(1)}, u32[]{:S(2)}, u32[]{:S(2)}) collective-permute-start(f32[3,1024]{0,1:T(8,128)S(1)} %slice.307), channel_id=1, source_target_pairs={{1,0},{2,1},{3,2},{4,3},{5,4},{6,5},{7,6},{9,8},{10,9},{11,10},{12... | collective-permute-start | bytes 36872 | tf_op jit(solution)/shard_map/ppermute | solution.py:15
